TPU v7x, 32 devices: a whole 2x2x4 slice. The times are simulated.
32 devices in a mesh: seg: 8 (over z, core), tok: 4 (over y, x).
Axes of the slice: x: 2, y: 2, z: 4, core: 2. Of those that a mesh axis runs over, the one named last changes fastest.
Arguments:
- queries: bfloat16 [2, 8, 2, 5120, 256], P(None, 'seg', None, 'tok'), may hold values from -6 to 6
- key_vectors: bfloat16 [2, 8, 2, 5120, 256], P(None, 'seg', None, 'tok'), may hold values from -6 to 6
- values: bfloat16 [2, 8, 2, 5120, 256], P(None, 'seg', None, 'tok'), may hold values from -6 to 6
- token_rates: float32 [2, 8, 2, 5120], P(None, 'seg', None, 'tok'), may hold values from 0.05 to 3
- fast_weights: float32 [8, 3, 256, 256], P('seg', None, None, 'tok'), may hold values from -0.375 to 0.375
- momenta: float32 [8, 3, 256, 256], P('seg', None, None, 'tok'), may hold values from -3 to 3
- fresh_weights: float32 [3, 256, 256], P(None, None, 'tok'), may hold values from -0.375 to 0.375
- fresh_momenta: float32 [3, 256, 256], P(None, None, 'tok'), may hold values from -3 to 3
Outputs:
- outputs: bfloat16 [2, 8, 2, 5120, 256], P(None, 'seg', None, 'tok')
- final_weights: float32 [8, 3, 256, 256], P('seg', None, None, 'tok')
- final_momenta: float32 [8, 3, 256, 256], P('seg', None, None, 'tok')
All inputs are finite; a program needn't handle non-finite values.
Results may differ from a plain program's by a relative error of at most 0.033.
Values may be sent and summed in bfloat16 or wider, within the bound.
A program may use at most 64 MiB of HBM per device.

v0:
```python
import jax
import jax.numpy as jnp
from jax import lax
from jax.sharding import PartitionSpec as P

momentum_decay = 0.9
learn_rate = 0.05
epsilon = 1e-06


def shifted(array, axis, by):
    length = lax.axis_size(axis)
    pairs = [(i, i + by) for i in range(length) if 0 <= i + by < length]
    return lax.ppermute(array, axis, pairs)


def silu_parts(pre_gate):
    sigmoid_gate = jax.nn.sigmoid(pre_gate)
    return (pre_gate * sigmoid_gate, sigmoid_gate * (1.0 + pre_gate * (1.0 - sigmoid_gate)))


def local_grads(usable_weights, key_rows, value_rows, rate_rows):
    pre_gate = jnp.dot(key_rows, usable_weights[0], preferred_element_type=jnp.float32)
    pre_up = jnp.dot(key_rows, usable_weights[2], preferred_element_type=jnp.float32)
    active, slope_gate = silu_parts(pre_gate)
    hidden = (active * pre_up).astype(jnp.bfloat16)
    scaled = (rate_rows[:, None] * value_rows.astype(jnp.float32)).astype(jnp.bfloat16)
    back_hidden = -lax.dot_general(
        scaled, usable_weights[1], (((1,), (1,)), ((), ())), preferred_element_type=jnp.float32
    )
    back_gate = (back_hidden * pre_up * slope_gate).astype(jnp.bfloat16)
    back_up = (back_hidden * active).astype(jnp.bfloat16)
    contract_rows = (((0,), (0,)), ((), ()))
    grad_gate = lax.dot_general(
        key_rows, back_gate, contract_rows, preferred_element_type=jnp.float32
    )
    grad_down = -lax.dot_general(hidden, scaled, contract_rows, preferred_element_type=jnp.float32)
    grad_up = lax.dot_general(key_rows, back_up, contract_rows, preferred_element_type=jnp.float32)
    return (jnp.stack([grad_gate, grad_down, grad_up]), jnp.sum(rate_rows * rate_rows))


def update(weights, moment, gradients, rate_total):
    moment = momentum_decay * moment + gradients * lax.rsqrt(rate_total)
    stepped = weights - learn_rate * moment
    rescale = jnp.sqrt(
        jnp.sum(weights * weights, axis=1, keepdims=True)
        / (jnp.sum(stepped * stepped, axis=1, keepdims=True) + epsilon)
    )
    return (stepped * rescale, moment)


def apply_fast(usable_weights, query_rows):
    pre_gate = jnp.dot(query_rows, usable_weights[0], preferred_element_type=jnp.float32)
    pre_up = jnp.dot(query_rows, usable_weights[2], preferred_element_type=jnp.float32)
    hidden = (jax.nn.silu(pre_gate) * pre_up).astype(jnp.bfloat16)
    return jnp.dot(hidden, usable_weights[1], preferred_element_type=jnp.float32).astype(
        jnp.bfloat16
    )


def usable(weights):
    rounded = weights.astype(jnp.bfloat16)
    return lax.all_gather(rounded, "tok", axis=2, tiled=True)


def advance(weights, moment, usable_weights, query_rows, key_rows, value_rows, rate_rows):
    gradients, square = local_grads(usable_weights, key_rows, value_rows, rate_rows)
    gradients = lax.psum_scatter(
        gradients.astype(jnp.bfloat16), "tok", scatter_dimension=2, tiled=True
    ).astype(jnp.float32)
    summed = lax.psum(square, "tok")
    weights, moment = update(weights, moment, gradients, summed)
    usable_weights = usable(weights)
    return (weights, moment, usable_weights, apply_fast(usable_weights, query_rows))


def body(
    queries, key_vectors, values, token_rates, fast_weights, momenta, fresh_weights, fresh_momenta
):
    sections = queries.shape[0]
    blocks = queries.shape[2]
    weights, moment, fresh_start, fresh_moment = (
        fast_weights[0],
        momenta[0],
        fresh_weights,
        fresh_momenta,
    )
    is_first = lax.axis_index("seg") == 0
    results = []
    for wave_step in range(sections):
        if wave_step > 0:
            passed = (
                shifted(weights.astype(jnp.bfloat16), "seg", 1).astype(weights.dtype),
                shifted(moment.astype(jnp.bfloat16), "seg", 1).astype(moment.dtype),
            )
            weights = jnp.where(is_first, fresh_start, passed[0])
            moment = jnp.where(is_first, fresh_moment, passed[1])
        usable_weights = usable(weights)
        for block_index in range(blocks):
            weights, moment, usable_weights, result = advance(
                weights,
                moment,
                usable_weights,
                queries[wave_step, 0, block_index],
                key_vectors[wave_step, 0, block_index],
                values[wave_step, 0, block_index],
                token_rates[wave_step, 0, block_index],
            )
            results.append(result)
    row_count = queries.shape[3]
    head_width = queries.shape[4]
    outputs = jnp.stack(results).reshape(sections, blocks, row_count, head_width)[:, None]
    return (outputs, weights[None], moment[None])


def solution(mesh):
    return jax.shard_map(
        body,
        mesh=mesh,
        in_specs=(
            P(None, "seg", None, "tok", None),
            P(None, "seg", None, "tok", None),
            P(None, "seg", None, "tok", None),
            P(None, "seg", None, "tok"),
            P("seg", None, None, "tok"),
            P("seg", None, None, "tok"),
            P(None, None, "tok"),
            P(None, None, "tok"),
        ),
        out_specs=(
            P(None, "seg", None, "tok", None),
            P("seg", None, None, "tok"),
            P("seg", None, None, "tok"),
        ),
        check_vma=False,
    )
```

profile of v0, /device:TPU:0, one launch (start us, length us, event | category | flops | bytes accessed | tf_op | source)
XLA Modules:
  0.0 212.2 jit_solution(14321896189256100010)
XLA Ops:
  8.3 11.0 %all_gather.18 = bf16[3,256,256]{1,2,0:T(8,128)(2,1)S(1)} all-gather(bf16[3,256,64]{1,2,0:T(8,128)(2,1)S(1)} %bitcast_convert_fusion), channel_id=1, replica_groups=mesh['seg'=8,'tok'=4] {'tok'}, dimensions={2}, use_global_device_ids=true | all-gather | bytes 491520 | tf_op jit(solution)/shard_map/all_gather | solution.py:63
  23.7 1.9 fusion.43
  28.5 9.6 %all-reduce = (f32[]{:T(128)}, f32[]{:T(128)}, f32[]{:T(128)}, f32[]{:T(128)}) all-reduce(f32[]{:T(128)} %get-tuple-element.34, f32[]{:T(128)} %get-tuple-element.33, f32[]{:T(128)} %get-tuple-element.32, f32[]{:T(128)} %get-tuple-element.31), channel_id=1, replica_groups=mesh['seg'=8,'tok'=4] {'tok'}, use_global_device_ids=true, to_apply=%region_2.0 | all-reduce | flops 4 | bytes 32 | tf_op jit(solution)/shard_map/psum | solution.py:71
  38.8 13.5 %reduce-scatter.5.cloned.1.call-done = bf16[3,256,64]{1,2,0:T(8,128)(2,1)} async-done(((bf16[3,256,256]{1,2,0:T(8,128)(2,1)}), bf16[3,256,64]{1,2,0:T(8,128)(2,1)}) %reduce-scatter.5.cloned.1.call-update) | async-done | bytes 98320 | tf_op jit(solution)/shard_map/reduce_scatter | solution.py:68
  53.5 9.9 %all_gather.19 = bf16[3,256,256]{1,2,0:T(8,128)(2,1)S(1)} all-gather(bf16[3,256,64]{1,2,0:T(8,128)(2,1)S(1)} %multiply_convert_fusion.27), channel_id=1, replica_groups=mesh['seg'=8,'tok'=4] {'tok'}, dimensions={2}, use_global_device_ids=true | all-gather | bytes 491520 | tf_op jit(solution)/shard_map/all_gather | solution.py:63
  66.2 1.9 fusion.42
  70.4 24.1 %reduce-scatter.7.cloned.1.call-done = bf16[3,256,64]{1,2,0:T(8,128)(2,1)} async-done(((bf16[3,256,256]{1,2,0:T(8,128)(2,1)}), bf16[3,256,64]{1,2,0:T(8,128)(2,1)}) %reduce-scatter.7.cloned.1.call-update) | async-done | bytes 98320 | tf_op jit(solution)/shard_map/reduce_scatter | solution.py:68
  94.5 1.7 multiply_reduce_fusion.4
  99.1 10.0 %all_gather.21 = bf16[3,256,256]{1,2,0:T(8,128)(2,1)S(1)} all-gather(bf16[3,256,64]{1,2,0:T(8,128)(2,1)S(1)} %fusion.145), channel_id=1, replica_groups=mesh['seg'=8,'tok'=4] {'tok'}, dimensions={2}, use_global_device_ids=true | all-gather | bytes 491520 | tf_op jit(solution)/shard_map/all_gather | solution.py:63
  111.9 1.9 fusion.41
  115.5 2.5 %convolution_bitcast_fusion.13 = f32[1280,256]{1,0:T(8,128)} fusion(bf16[2,1,2,1280,256]{4,3,2,1,0:T(8,128)(2,1)} %param.8, bf16[3,256,256]{1,2,0:T(8,128)(2,1)S(1)} %all_gather.19), kind=kOutput, calls=%fused_computation.20 | convolution fusion | flops 167772160 | bytes 2097152 | tf_op jit(solution)/shard_map/dot_general | solution.py:53
  118.0 3.0 %fusion.8 = bf16[1,1280,256]{2,1,0:T(8,128)(2,1)} fusion(f32[1280,256]{1,0:T(8,128)} %convolution_bitcast_fusion.13, bf16[2,1,2,1280,256]{4,3,2,1,0:T(8,128)(2,1)} %param.8, bf16[3,256,256]{1,2,0:T(8,128)(2,1)S(1)} %all_gather.19), kind=kOutput, calls=%fused_computation.31 | convolution fusion | flops 337838080 | bytes 2883584 | tf_op jit(solution)/shard_map/dot_general | solution.py:56
  121.0 2.3 %collective-permute-start.1 = (bf16[3,256,64]{1,2,0:T(8,128)(2,1)}, bf16[3,256,64]{1,2,0:T(8,128)(2,1)S(1)}, u32[]{:S(2)}, u32[]{:S(2)}) collective-permute-start(bf16[3,256,64]{1,2,0:T(8,128)(2,1)} %get-tuple-element.23), channel_id=1, source_target_pairs={{0,4},{4,8},{8,12},{12,16},{16,20},{20,24},{24,28},{1,5},{5,9},{9,... | collective-permute-start | bytes 294920 | tf_op jit(solution)/shard_map/ppermute | solution.py:14
  123.3 10.1 %all_gather.20 = bf16[3,256,256]{1,2,0:T(8,128)(2,1)S(1)} all-gather(bf16[3,256,64]{1,2,0:T(8,128)(2,1)S(1)} %multiply_convert_fusion.24), channel_id=1, replica_groups=mesh['seg'=8,'tok'=4] {'tok'}, dimensions={2}, use_global_device_ids=true | all-gather | bytes 491520 | tf_op jit(solution)/shard_map/all_gather | solution.py:63
  133.3 2.7 %convolution_bitcast_fusion.9 = f32[1280,256]{1,0:T(8,128)} fusion(bf16[2,1,2,1280,256]{4,3,2,1,0:T(8,128)(2,1)} %param.8, bf16[3,256,256]{1,2,0:T(8,128)(2,1)S(1)} %all_gather.20), kind=kOutput, calls=%fused_computation.14 | convolution fusion | flops 167772160 | bytes 2097152 | tf_op jit(solution)/shard_map/dot_general | solution.py:53
  136.0 7.1 %reduce-scatter.9.cloned.1.call-done = bf16[3,256,64]{1,2,0:T(8,128)(2,1)} async-done(((bf16[3,256,256]{1,2,0:T(8,128)(2,1)}), bf16[3,256,64]{1,2,0:T(8,128)(2,1)}) %reduce-scatter.9.cloned.1.call-update) | async-done | bytes 98320 | tf_op jit(solution)/shard_map/reduce_scatter | solution.py:68
  144.4 10.2 %all_gather.22 = bf16[3,256,256]{1,2,0:T(8,128)(2,1)S(1)} all-gather(bf16[3,256,64]{1,2,0:T(8,128)(2,1)S(1)} %multiply_convert_fusion.26), channel_id=1, replica_groups=mesh['seg'=8,'tok'=4] {'tok'}, dimensions={2}, use_global_device_ids=true | all-gather | bytes 491520 | tf_op jit(solution)/shard_map/all_gather | solution.py:63
  157.4 1.9 fusion.40
  160.9 3.2 %fusion.9 = bf16[1,1280,256]{2,1,0:T(8,128)(2,1)} fusion(f32[1280,256]{1,0:T(8,128)} %convolution_bitcast_fusion.9, bf16[2,1,2,1280,256]{4,3,2,1,0:T(8,128)(2,1)} %param.8, bf16[3,256,256]{1,2,0:T(8,128)(2,1)} %copy-done.5), kind=kOutput, calls=%fused_computation.32 | convolution fusion | flops 337838080 | bytes 2883584 | tf_op jit(solution)/shard_map/dot_general | solution.py:56
  165.5 2.8 %fusion.10 = bf16[1,1280,256]{2,1,0:T(8,128)(2,1)} fusion(f32[1280,256]{1,0:T(8,128)} %convolution_bitcast_fusion.5, bf16[2,1,2,1280,256]{4,3,2,1,0:T(8,128)(2,1)S(1)} %copy-done.1, bf16[3,256,256]{1,2,0:T(8,128)(2,1)S(1)} %all_gather.22), kind=kOutput, calls=%fused_computation.33 | convolution fusion | flops 337838080 | bytes 2883584 | tf_op jit(solution)/shard_map/dot_general | solution.py:56
  168.3 17.3 %reduce-scatter.11.cloned.1.call-done = bf16[3,256,64]{1,2,0:T(8,128)(2,1)} async-done(((bf16[3,256,256]{1,2,0:T(8,128)(2,1)}), bf16[3,256,64]{1,2,0:T(8,128)(2,1)}) %reduce-scatter.11.cloned.1.call-update) | async-done | bytes 98320 | tf_op jit(solution)/shard_map/reduce_scatter | solution.py:68
  188.1 9.9 %all_gather.23 = bf16[3,256,256]{1,2,0:T(8,128)(2,1)S(1)} all-gather(bf16[3,256,64]{1,2,0:T(8,128)(2,1)S(1)} %get-tuple-element.29), channel_id=1, replica_groups=mesh['seg'=8,'tok'=4] {'tok'}, dimensions={2}, use_global_device_ids=true | all-gather | bytes 491520 | tf_op jit(solution)/shard_map/all_gather | solution.py:63
  199.4 2.8 %fusion.11 = bf16[1,1280,256]{2,1,0:T(8,128)(2,1)} fusion(f32[1280,256]{1,0:T(8,128)} %convolution_bitcast_fusion.1, bf16[2,1,2,1280,256]{4,3,2,1,0:T(8,128)(2,1)S(1)} %copy-done.1, bf16[3,256,256]{1,2,0:T(8,128)(2,1)S(1)} %all_gather.23), kind=kOutput, calls=%fused_computation.34 | convolution fusion | flops 337838080 | bytes 2883584 | tf_op jit(solution)/shard_map/dot_general | solution.py:56
  202.2 3.5 %pad_maximum_fusion = bf16[4,1280,256]{2,1,0:T(8,128)(2,1)} fusion(bf16[1,1280,256]{2,1,0:T(8,128)(2,1)} %fusion.11, bf16[1,1280,256]{2,1,0:T(8,128)(2,1)} %fusion.10, bf16[1,1280,256]{2,1,0:T(8,128)(2,1)} %fusion.9, bf16[1,1280,256]{2,1,0:T(8,128)(2,1)} %fusion.8), kind=kLoop, calls=%fused_computation.22 | loop fusion | flops 3932160 | bytes 5242880 | tf_op jit(solution)/shard_map/stack | solution.py:112
  (69 shorter events, 30.7 us)
Async XLA Ops:
  7.2 45.1 %reduce-scatter.5.cloned.1.call-start = ((), (), s32[]{:S(2)}) async-start(), calls=%async_computation.4 | async-start | bytes 491520 | tf_op jit(solution)/shard_map/reduce_scatter | solution.py:68
  7.2 13.5 %copy-start = (bf16[2,1,2,1280,256]{4,3,2,1,0:T(8,128)(2,1)S(1)}, bf16[2,1,2,1280,256]{4,3,2,1,0:T(8,128)(2,1)}, u32[]{:S(2)}) copy-start(bf16[2,1,2,1280,256]{4,3,2,1,0:T(8,128)(2,1)} %param.9) | copy-start | bytes 7864324
  20.8 0.7 copy-start.7
  26.3 26.0 %copy-start.3 = (f32[1,3,256,64]{2,3,1,0:T(8,128)S(1)}, f32[1,3,256,64]{2,3,1,0:T(8,128)}, u32[]{:S(2)}) copy-start(f32[1,3,256,64]{2,3,1,0:T(8,128)} %param.12) | copy-start | bytes 589828
  26.3 26.0 %copy-start.4 = (f32[1,3,256,64]{2,3,1,0:T(8,128)S(1)}, f32[1,3,256,64]{2,3,1,0:T(8,128)}, u32[]{:S(2)}) copy-start(f32[1,3,256,64]{2,3,1,0:T(8,128)} %param.13) | copy-start | bytes 589828
  27.1 67.4 %reduce-scatter.7.cloned.1.call-start = ((), (), s32[]{:S(2)}) async-start(), calls=%async_computation.5 | async-start | bytes 491520 | tf_op jit(solution)/shard_map/reduce_scatter | solution.py:68
  68.1 26.4 %copy-start.6 = (bf16[3,256,64]{1,2,0:T(8,128)(2,1)S(1)}, bf16[3,256,64]{1,2,0:T(8,128)(2,1)}, u32[]{:S(2)}) copy-start(bf16[3,256,64]{1,2,0:T(8,128)(2,1)} %reduce-scatter.5.cloned.1.call-done) | copy-start | bytes 294916
  68.9 30.2 %copy-start.2 = (f32[3,256,64]{1,2,0:T(8,128)S(1)}, f32[3,256,64]{1,2,0:T(8,128)}, u32[]{:S(2)}) copy-start(f32[3,256,64]{1,2,0:T(8,128)} %param.14) | copy-start | bytes 589828
  69.7 73.4 %reduce-scatter.9.cloned.1.call-start = ((), (), s32[]{:S(2)}) async-start(), calls=%async_computation.6 | async-start | bytes 491520 | tf_op jit(solution)/shard_map/reduce_scatter | solution.py:68
  96.4 2.6 %collective-permute-start = (bf16[3,256,64]{1,2,0:T(8,128)(2,1)S(1)}, bf16[3,256,64]{1,2,0:T(8,128)(2,1)S(1)}, u32[]{:S(2)}, u32[]{:S(2)}) collective-permute-start(bf16[3,256,64]{1,2,0:T(8,128)(2,1)S(1)} %multiply_convert_fusion.24), channel_id=1, source_target_pairs={{0,4},{4,8},{8,12},{12,16},{16,20},{20,24},{24,28},{1,5},{5,9},{9,... | collective-permute-start | bytes 294920 | tf_op jit(solution)/shard_map/ppermute | solution.py:14
  115.4 70.2 %reduce-scatter.11.cloned.1.call-start = ((), (), s32[]{:S(2)}) async-start(), calls=%async_computation.7 | async-start | bytes 491520 | tf_op jit(solution)/shard_map/reduce_scatter | solution.py:68
  121.0 15.0 %collective-permute-start.1 = (bf16[3,256,64]{1,2,0:T(8,128)(2,1)}, bf16[3,256,64]{1,2,0:T(8,128)(2,1)S(1)}, u32[]{:S(2)}, u32[]{:S(2)}) collective-permute-start(bf16[3,256,64]{1,2,0:T(8,128)(2,1)} %get-tuple-element.23), channel_id=1, source_target_pairs={{0,4},{4,8},{8,12},{12,16},{16,20},{20,24},{24,28},{1,5},{5,9},{9,... | collective-permute-start | bytes 294920 | tf_op jit(solution)/shard_map/ppermute | solution.py:14
  133.3 2.7 %copy-start.5 = (bf16[3,256,256]{1,2,0:T(8,128)(2,1)}, bf16[3,256,256]{1,2,0:T(8,128)(2,1)S(1)}, u32[]{:S(2)}) copy-start(bf16[3,256,256]{1,2,0:T(8,128)(2,1)S(1)} %all_gather.20) | copy-start | bytes 1179652
  160.9 3.2 %copy-start.1 = (bf16[2,1,2,1280,256]{4,3,2,1,0:T(8,128)(2,1)S(1)}, bf16[2,1,2,1280,256]{4,3,2,1,0:T(8,128)(2,1)}, u32[]{:S(2)}) copy-start(bf16[2,1,2,1280,256]{4,3,2,1,0:T(8,128)(2,1)} %param.8) | copy-start | bytes 7864324
Sparse Core Ops, SparseCore 0:
  27.3 24.9 reduce-scatter.4
  69.8 24.6 reduce-scatter.6
  115.5 27.5 reduce-scatter.8
  161.0 24.5 reduce-scatter.10
where the time goes:
time: 213 us; the launch traced here: 212 us
  blocking collectives  70.7 us (33%)
  waiting for transfers between devices  62 us (29%)
  matrix products  42.7 us (20%)
  between operations  16.8 us (8%)
  other arithmetic  15.8 us (7%)
  starting transfers between devices  3.74 us (2%)
    reduce_scatter x4, waiting for transfers between devices, advance(): lax.psum_scatter(gradients.astype(jnp.bfloat16), 'tok', scatter_dimension...  61.9 us
    all_gather x6, blocking collectives, usable(): return lax.all_gather(rounded, 'tok', axis=2, tiled=True)  61.1 us
    dot_general x4, matrix products, apply_fast(): jnp.dot(hidden, usable_weights[1], preferred_element_type=jnp.float32)  11.8 us
    psum x1, blocking collectives, advance(): summed = lax.psum(square, 'tok')  9.65 us
    dot_general x4, matrix products, apply_fast(): jnp.dot(query_rows, usable_weights[0], preferred_element_type=jnp.float32)  8 us
    dot_general x4, matrix products, local_grads(): lax.dot_general(hidden, scaled, contract_rows, preferred_element_type=jnp...  7.57 us
    dot_general x4, matrix products, local_grads(): lax.dot_general(scaled, usable_weights[1], (((1,), (1,)), ((), ())), pref...  5.9 us
    reduce_sum x4, other arithmetic, update(): jnp.sum(stepped * stepped, axis=1, keepdims=True) + epsilon  5.57 us
  transfers between devices with their start and end apart: 6, of which 4 were waited for; matrix products, arithmetic and copies ran while one was open for 8% of the time, Pallas kernels for 0%

commit v1 on v0

--- a/solution.py
+++ b/solution.py
@@ -6,6 +6,11 @@
 momentum_decay = 0.9
 learn_rate = 0.05
 epsilon = 1e-06
+
+
+def all_parts(x, axis, dim):
+    blocks = lax.all_gather(x, axis)
+    return jnp.concatenate(blocks, axis=dim)
 
 
 def shifted(array, axis, by):
@@ -60,7 +65,7 @@
 
 def usable(weights):
     rounded = weights.astype(jnp.bfloat16)
-    return lax.all_gather(rounded, "tok", axis=2, tiled=True)
+    return all_parts(rounded, "tok", 2)
 
 
 def advance(weights, moment, usable_weights, query_rows, key_rows, value_rows, rate_rows):

time: 213 us -> 210 us (0.986)
  matrix products: 42.7 us -> 38.5 us
  local copies, waits for them, and re-layouts: 0.45 us -> 2.7 us
    dot_general x4, matrix products: 7.57 us -> 5.38 us  [local_grads(): lax.dot_general(hidden, scaled, contract_rows, preferred_element_type=jnp...]
    dot_general x4, matrix products: 5.9 us -> 3.72 us  [local_grads(): lax.dot_general(scaled, usable_weights[1], (((1,), (1,)), ((), ())), pref...]
where the time goes in v1:
time: 210 us; the launch traced here: 209 us
  blocking collectives  71.7 us (34%)
  waiting for transfers between devices  60.1 us (29%)
  matrix products  38.5 us (18%)
  between operations  16.8 us (8%)
  other arithmetic  15.5 us (7%)
  starting transfers between devices  3.49 us (2%)
  local copies, waits for them, and re-layouts  2.7 us (1%)
    all_gather x6, blocking collectives, all_parts(): blocks = lax.all_gather(x, axis)  62 us
    reduce_scatter x4, waiting for transfers between devices, advance(): lax.psum_scatter(gradients.astype(jnp.bfloat16), 'tok', scatter_dimension...  60 us
    dot_general x4, matrix products, apply_fast(): jnp.dot(hidden, usable_weights[1], preferred_element_type=jnp.float32)  11.9 us
    psum x1, blocking collectives, advance(): summed = lax.psum(square, 'tok')  9.66 us
    dot_general x4, matrix products, apply_fast(): jnp.dot(query_rows, usable_weights[0], preferred_element_type=jnp.float32)  8 us
    reduce_sum x4, other arithmetic, update(): jnp.sum(stepped * stepped, axis=1, keepdims=True) + epsilon  5.65 us
    dot_general x4, matrix products, local_grads(): lax.dot_general(hidden, scaled, contract_rows, preferred_element_type=jnp...  5.38 us
  transfers between devices with their start and end apart: 6, of which 4 were waited for; matrix products, arithmetic and copies ran while one was open for 8% of the time, Pallas kernels for 0%

profile of v1, /device:TPU:0, one launch (start us, length us, event | category | flops | bytes accessed | tf_op | source)
XLA Modules:
  0.0 208.8 jit_solution(4460492597925444642)
XLA Ops:
  9.0 11.0 %all_gather.34 = bf16[4,3,256,64]{2,3,1,0:T(8,128)(2,1)S(1)} all-gather(bf16[1,3,256,64]{2,3,1,0:T(8,128)(2,1)S(1)} %convert_element_type.176), channel_id=1, replica_groups=mesh['seg'=8,'tok'=4] {'tok'}, dimensions={0}, use_global_device_ids=true | all-gather | bytes 491520 | tf_op jit(solution)/shard_map/all_gather | solution.py:12
  20.0 1.6 fusion.82
  24.4 1.9 fusion.43
  29.2 9.7 %all-reduce = (f32[]{:T(128)}, f32[]{:T(128)}, f32[]{:T(128)}, f32[]{:T(128)}) all-reduce(f32[]{:T(128)} %get-tuple-element.55, f32[]{:T(128)} %get-tuple-element.54, f32[]{:T(128)} %get-tuple-element.53, f32[]{:T(128)} %get-tuple-element.52), channel_id=1, replica_groups=mesh['seg'=8,'tok'=4] {'tok'}, use_global_device_ids=true, to_apply=%region_2.0 | all-reduce | flops 4 | bytes 32 | tf_op jit(solution)/shard_map/psum | solution.py:76
  39.6 13.5 %reduce-scatter.5.cloned.1.call-done = bf16[3,256,64]{1,2,0:T(8,128)(2,1)} async-done(((bf16[3,256,256]{1,2,0:T(8,128)(2,1)}), bf16[3,256,64]{1,2,0:T(8,128)(2,1)}) %reduce-scatter.5.cloned.1.call-update) | async-done | bytes 98320 | tf_op jit(solution)/shard_map/reduce_scatter | solution.py:73
  54.2 9.9 %all-gather = bf16[12,256,64]{1,2,0:T(8,128)(2,1)S(1)} all-gather(bf16[3,256,64]{1,2,0:T(8,128)(2,1)S(1)} %multiply_convert_fusion.27), channel_id=2, replica_groups=mesh['seg'=8,'tok'=4] {'tok'}, dimensions={0}, use_global_device_ids=true | all-gather | bytes 491520 | tf_op jit(solution)/shard_map/all_gather | solution.py:12
  67.0 1.9 fusion.42
  72.5 22.9 %reduce-scatter.7.cloned.1.call-done = bf16[3,256,64]{1,2,0:T(8,128)(2,1)} async-done(((bf16[3,256,256]{1,2,0:T(8,128)(2,1)}), bf16[3,256,64]{1,2,0:T(8,128)(2,1)}) %reduce-scatter.7.cloned.1.call-update) | async-done | bytes 98320 | tf_op jit(solution)/shard_map/reduce_scatter | solution.py:73
  95.4 1.7 multiply_reduce_fusion.4
  98.5 2.7 %convolution_bitcast_fusion.13 = f32[1280,256]{1,0:T(8,128)} fusion(bf16[256,256]{0,1:T(8,128)(2,1)S(1)} %bitcast.289, bf16[2,1,2,1280,256]{4,3,2,1,0:T(8,128)(2,1)} %param.8), kind=kOutput, calls=%fused_computation.20 | convolution fusion | flops 167772160 | bytes 2097152 | tf_op jit(solution)/shard_map/dot_general | solution.py:58
  101.2 10.3 %all-gather.2 = bf16[12,256,64]{1,2,0:T(8,128)(2,1)S(1)} all-gather(bf16[3,256,64]{1,2,0:T(8,128)(2,1)S(1)} %fusion.145), channel_id=4, replica_groups=mesh['seg'=8,'tok'=4] {'tok'}, dimensions={0}, use_global_device_ids=true | all-gather | bytes 491520 | tf_op jit(solution)/shard_map/all_gather | solution.py:12
  115.7 3.0 %fusion.8 = bf16[1,1280,256]{2,1,0:T(8,128)(2,1)} fusion(bf16[256,256]{0,1:T(8,128)(2,1)S(1)} %bitcast.295, bf16[256,256]{0,1:T(8,128)(2,1)S(1)} %bitcast.293, f32[1280,256]{1,0:T(8,128)} %convolution_bitcast_fusion.13, bf16[2,1,2,1280,256]{4,3,2,1,0:T(8,128)(2,1)} %param.8), kind=kOutput, calls=%fused_computation.31 | convolution fusion | flops 337838080 | bytes 2883584 | tf_op jit(solution)/shard_map/dot_general | solution.py:61
  118.7 2.0 collective-permute-start.1
  120.7 10.8 %all-gather.1 = bf16[12,256,64]{1,2,0:T(8,128)(2,1)S(1)} all-gather(bf16[3,256,64]{1,2,0:T(8,128)(2,1)S(1)} %multiply_convert_fusion.24), channel_id=3, replica_groups=mesh['seg'=8,'tok'=4] {'tok'}, dimensions={0}, use_global_device_ids=true | all-gather | bytes 491520 | tf_op jit(solution)/shard_map/all_gather | solution.py:12
  132.2 2.5 %convolution_bitcast_fusion.9 = f32[1280,256]{1,0:T(8,128)} fusion(bf16[256,256]{0,1:T(8,128)(2,1)S(1)} %bitcast.306, bf16[2,1,2,1280,256]{4,3,2,1,0:T(8,128)(2,1)} %param.8), kind=kOutput, calls=%fused_computation.14 | convolution fusion | flops 167772160 | bytes 2097152 | tf_op jit(solution)/shard_map/dot_general | solution.py:58
  135.4 6.3 %reduce-scatter.9.cloned.1.call-done = bf16[3,256,64]{1,2,0:T(8,128)(2,1)} async-done(((bf16[3,256,256]{1,2,0:T(8,128)(2,1)}), bf16[3,256,64]{1,2,0:T(8,128)(2,1)}) %reduce-scatter.9.cloned.1.call-update) | async-done | bytes 98320 | tf_op jit(solution)/shard_map/reduce_scatter | solution.py:73
  143.1 10.1 %all-gather.3 = bf16[12,256,64]{1,2,0:T(8,128)(2,1)S(1)} all-gather(bf16[3,256,64]{1,2,0:T(8,128)(2,1)S(1)} %multiply_convert_fusion.26), channel_id=5, replica_groups=mesh['seg'=8,'tok'=4] {'tok'}, dimensions={0}, use_global_device_ids=true | all-gather | bytes 491520 | tf_op jit(solution)/shard_map/all_gather | solution.py:12
  157.5 3.2 %fusion.9 = bf16[1,1280,256]{2,1,0:T(8,128)(2,1)} fusion(bf16[256,256]{0,1:T(8,128)(2,1)} %bitcast.308, bf16[256,256]{0,1:T(8,128)(2,1)} %bitcast.309, f32[1280,256]{1,0:T(8,128)} %convolution_bitcast_fusion.9, bf16[2,1,2,1280,256]{4,3,2,1,0:T(8,128)(2,1)} %param.8), kind=kOutput, calls=%fused_computation.32 | convolution fusion | flops 337838080 | bytes 2883584 | tf_op jit(solution)/shard_map/dot_general | solution.py:61
  162.1 2.8 %fusion.10 = bf16[1,1280,256]{2,1,0:T(8,128)(2,1)} fusion(bf16[256,256]{0,1:T(8,128)(2,1)S(1)} %bitcast.299, bf16[256,256]{0,1:T(8,128)(2,1)S(1)} %bitcast.297, f32[1280,256]{1,0:T(8,128)} %convolution_bitcast_fusion.5, bf16[2,1,2,1280,256]{4,3,2,1,0:T(8,128)(2,1)S(1)} %copy-done.3), kind=kOutput, calls=%fused_computation.33 | convolution fusion | flops 337838080 | bytes 2883584 | tf_op jit(solution)/shard_map/dot_general | solution.py:61
  164.9 17.4 %reduce-scatter.11.cloned.1.call-done = bf16[3,256,64]{1,2,0:T(8,128)(2,1)} async-done(((bf16[3,256,256]{1,2,0:T(8,128)(2,1)}), bf16[3,256,64]{1,2,0:T(8,128)(2,1)}) %reduce-scatter.11.cloned.1.call-update) | async-done | bytes 98320 | tf_op jit(solution)/shard_map/reduce_scatter | solution.py:73
  182.3 1.7 multiply_reduce_fusion
  184.7 9.9 %all-gather.4 = bf16[12,256,64]{1,2,0:T(8,128)(2,1)S(1)} all-gather(bf16[3,256,64]{1,2,0:T(8,128)(2,1)S(1)} %get-tuple-element.50), channel_id=6, replica_groups=mesh['seg'=8,'tok'=4] {'tok'}, dimensions={0}, use_global_device_ids=true | all-gather | bytes 491520 | tf_op jit(solution)/shard_map/all_gather | solution.py:12
  196.1 2.9 %fusion.11 = bf16[1,1280,256]{2,1,0:T(8,128)(2,1)} fusion(bf16[256,256]{0,1:T(8,128)(2,1)S(1)} %bitcast.310, bf16[256,256]{0,1:T(8,128)(2,1)S(1)} %bitcast.311, f32[1280,256]{1,0:T(8,128)} %convolution_bitcast_fusion.1, bf16[2,1,2,1280,256]{4,3,2,1,0:T(8,128)(2,1)S(1)} %copy-done.3), kind=kOutput, calls=%fused_computation.34 | convolution fusion | flops 337838080 | bytes 2883584 | tf_op jit(solution)/shard_map/dot_general | solution.py:61
  199.0 3.3 %pad_maximum_fusion = bf16[4,1280,256]{2,1,0:T(8,128)(2,1)} fusion(bf16[1,1280,256]{2,1,0:T(8,128)(2,1)} %fusion.11, bf16[1,1280,256]{2,1,0:T(8,128)(2,1)} %fusion.10, bf16[1,1280,256]{2,1,0:T(8,128)(2,1)} %fusion.9, bf16[1,1280,256]{2,1,0:T(8,128)(2,1)S(1)} %copy-done.7), kind=kLoop, calls=%fused_computation.22 | loop fusion | flops 3932160 | bytes 5242880 | tf_op jit(solution)/shard_map/stack | solution.py:117
  (83 shorter events, 29.2 us)
Async XLA Ops:
  7.2 45.9 %reduce-scatter.5.cloned.1.call-start = ((), (), s32[]{:S(2)}) async-start(), calls=%async_computation.4 | async-start | bytes 491520 | tf_op jit(solution)/shard_map/reduce_scatter | solution.py:73
  20.0 1.9 copy-start
  27.0 26.0 %copy-start.5 = (f32[1,3,256,64]{2,3,1,0:T(8,128)S(1)}, f32[1,3,256,64]{2,3,1,0:T(8,128)}, u32[]{:S(2)}) copy-start(f32[1,3,256,64]{2,3,1,0:T(8,128)} %param.12) | copy-start | bytes 589828
  27.0 26.0 %copy-start.6 = (f32[1,3,256,64]{2,3,1,0:T(8,128)S(1)}, f32[1,3,256,64]{2,3,1,0:T(8,128)}, u32[]{:S(2)}) copy-start(f32[1,3,256,64]{2,3,1,0:T(8,128)} %param.13) | copy-start | bytes 589828
  27.9 67.5 %reduce-scatter.7.cloned.1.call-start = ((), (), s32[]{:S(2)}) async-start(), calls=%async_computation.5 | async-start | bytes 491520 | tf_op jit(solution)/shard_map/reduce_scatter | solution.py:73
  70.4 71.3 %reduce-scatter.9.cloned.1.call-start = ((), (), s32[]{:S(2)}) async-start(), calls=%async_computation.6 | async-start | bytes 491520 | tf_op jit(solution)/shard_map/reduce_scatter | solution.py:73
  97.0 4.1 %copy-start.4 = (f32[3,256,64]{1,2,0:T(8,128)S(1)}, f32[3,256,64]{1,2,0:T(8,128)}, u32[]{:S(2)}) copy-start(f32[3,256,64]{1,2,0:T(8,128)} %param.14) | copy-start | bytes 589828
  97.2 4.0 %collective-permute-start = (bf16[3,256,64]{1,2,0:T(8,128)(2,1)S(1)}, bf16[3,256,64]{1,2,0:T(8,128)(2,1)S(1)}, u32[]{:S(2)}, u32[]{:S(2)}) collective-permute-start(bf16[3,256,64]{1,2,0:T(8,128)(2,1)S(1)} %multiply_convert_fusion.24), channel_id=1, source_target_pairs={{0,4},{4,8},{8,12},{12,16},{16,20},{20,24},{24,28},{1,5},{5,9},{9,... | collective-permute-start | bytes 294920 | tf_op jit(solution)/shard_map/ppermute | solution.py:19
  98.5 13.0 %copy-start.1 = (bf16[2,1,2,1280,256]{4,3,2,1,0:T(8,128)(2,1)S(1)}, bf16[2,1,2,1280,256]{4,3,2,1,0:T(8,128)(2,1)}, u32[]{:S(2)}) copy-start(bf16[2,1,2,1280,256]{4,3,2,1,0:T(8,128)(2,1)} %param.10) | copy-start | bytes 7864324
  101.1 10.3 %copy-start.8 = (bf16[3,256,64]{1,2,0:T(8,128)(2,1)}, bf16[3,256,64]{1,2,0:T(8,128)(2,1)S(1)}, u32[]{:S(2)}) copy-start(bf16[3,256,64]{1,2,0:T(8,128)(2,1)S(1)} %collective-permute-done) | copy-start | bytes 294916
  115.6 66.6 %reduce-scatter.11.cloned.1.call-start = ((), (), s32[]{:S(2)}) async-start(), calls=%async_computation.7 | async-start | bytes 491520 | tf_op jit(solution)/shard_map/reduce_scatter | solution.py:73
  118.7 16.1 %collective-permute-start.1 = (bf16[3,256,64]{1,2,0:T(8,128)(2,1)}, bf16[3,256,64]{1,2,0:T(8,128)(2,1)S(1)}, u32[]{:S(2)}, u32[]{:S(2)}) collective-permute-start(bf16[3,256,64]{1,2,0:T(8,128)(2,1)} %get-tuple-element.35), channel_id=1, source_target_pairs={{0,4},{4,8},{8,12},{12,16},{16,20},{20,24},{24,28},{1,5},{5,9},{9,... | collective-permute-start | bytes 294920 | tf_op jit(solution)/shard_map/ppermute | solution.py:19
  131.5 10.2 %copy-start.9 = (bf16[3,256,64]{1,2,0:T(8,128)(2,1)S(1)}, bf16[3,256,64]{1,2,0:T(8,128)(2,1)}, u32[]{:S(2)}) copy-start(bf16[3,256,64]{1,2,0:T(8,128)(2,1)} %copy-done.8) | copy-start | bytes 294916
  131.5 10.2 %copy-start.10 = (f32[3,256,64]{1,2,0:T(8,128)S(1)}, f32[3,256,64]{1,2,0:T(8,128)}, u32[]{:S(2)}) copy-start(f32[3,256,64]{1,2,0:T(8,128)} %param.15) | copy-start | bytes 589828
  134.8 0.6 copy-start.11
  141.8 11.5 %copy-start.2 = (bf16[2,1,2,1280,256]{4,3,2,1,0:T(8,128)(2,1)S(1)}, bf16[2,1,2,1280,256]{4,3,2,1,0:T(8,128)(2,1)}, u32[]{:S(2)}) copy-start(bf16[2,1,2,1280,256]{4,3,2,1,0:T(8,128)(2,1)} %param.10) | copy-start | bytes 7864324
  157.5 3.2 %copy-start.3 = (bf16[2,1,2,1280,256]{4,3,2,1,0:T(8,128)(2,1)S(1)}, bf16[2,1,2,1280,256]{4,3,2,1,0:T(8,128)(2,1)}, u32[]{:S(2)}) copy-start(bf16[2,1,2,1280,256]{4,3,2,1,0:T(8,128)(2,1)} %param.8) | copy-start | bytes 7864324
  196.1 2.9 %copy-start.7 = (bf16[1,1280,256]{2,1,0:T(8,128)(2,1)S(1)}, bf16[1,1280,256]{2,1,0:T(8,128)(2,1)}, u32[]{:S(2)}) copy-start(bf16[1,1280,256]{2,1,0:T(8,128)(2,1)} %fusion.8) | copy-start | bytes 1966084
Sparse Core Ops, SparseCore 0:
  28.0 24.9 reduce-scatter.4
  70.6 24.7 reduce-scatter.6
  115.8 25.9 reduce-scatter.8
  157.6 24.6 reduce-scatter.10
